TPU v7x, 32 devices: a whole 2x2x4 slice. The times are simulated.
32 devices in a mesh: row: 8 (over z, y), col: 4 (over x, core).
Axes of the slice: x: 2, y: 2, z: 4, core: 2. Of those that a mesh axis runs over, the one named last changes fastest.
Arguments:
- tracer: float32 [128, 128, 512], P(None, 'row', 'col'), may hold values from -6 to 6
- symbol_x: float32 [128], replicated, may hold values from 0.3 to 3
- symbol_y: float32 [128], replicated, may hold values from 0.3 to 3
- symbol_z: float32 [512], replicated, may hold values from 0.3 to 3
Outputs:
- spectrum: float32 [128, 128, 512], P('row', 'col')
All inputs are finite; a program needn't handle non-finite values.
Results may differ from a plain program's by a relative error of at most 0.000075.
Values sent between devices are 32-bit elements; how exact they have to be, the bound alone decides.
No kernel may reach another device: no remote copies, remote signals or barrier semaphores. Data moves between devices by JAX's collectives and lax.ppermute only.
A program may use at most 64 MiB of HBM per device.

v0:
```python
import jax
import jax.numpy as jnp
from jax import lax
from jax.sharding import PartitionSpec as P


def transform_table(count):
    rank = jnp.arange(count)
    angle = (
        jnp.pi
        / (count + 1)
        * ((rank[:, None] + 1) * (rank[None, :] + 1) % (2 * count + 2)).astype(jnp.float32)
    )
    return jnp.sin(angle) * (2.0 / (count + 1)) ** 0.5


def to_modes(values, dim):
    moved = jnp.tensordot(
        values,
        transform_table(values.shape[dim]),
        axes=([dim], [0]),
        precision=lax.Precision.HIGHEST,
    )
    return jnp.moveaxis(moved, -1, dim)


def per_device(tracer, symbol_x, symbol_y, symbol_z):
    part_values = tracer
    part_values = to_modes(part_values, 0)
    part_values = lax.all_to_all(part_values, "row", split_axis=0, concat_axis=1, tiled=True)
    part_values = to_modes(part_values, 1)
    local_values = part_values
    local_values = lax.all_to_all(local_values, "col", split_axis=1, concat_axis=2, tiled=True)
    local_values = to_modes(local_values, 2)
    share_x = local_values.shape[0]
    part_x = lax.dynamic_slice_in_dim(symbol_x, lax.axis_index("row") * share_x, share_x)
    share_y = local_values.shape[1]
    part_y = lax.dynamic_slice_in_dim(symbol_y, lax.axis_index("col") * share_y, share_y)
    symbol = part_x[:, None, None] + part_y[None, :, None] + symbol_z[None, None, :]
    local_values = local_values * ((1.0 - 0.2 * symbol) / (1.0 + 0.2 * symbol))
    return local_values


def solution(mesh):
    in_specs = (P(None, "row", "col"), P(), P(), P())
    out_specs = P("row", "col", None)
    return jax.shard_map(
        per_device, mesh=mesh, in_specs=in_specs, out_specs=out_specs, check_vma=False
    )
```

profile of v0, /device:TPU:0, one launch (start us, length us, event | category | flops | bytes accessed | tf_op | source)
XLA Modules:
  0.0 66.0 jit_solution(14999294112049493810)
XLA Ops:
  0.0 0.0 copy-start
  0.0 1.2 %copy-done = f32[128,16,128]{2,1,0:T(8,128)S(1)} copy-done((f32[128,16,128]{2,1,0:T(8,128)S(1)}, f32[128,16,128]{2,1,0:T(8,128)}, u32[]{:S(2)}) %copy-start) | copy-done | bytes 1048600
  1.2 1.6 %fusion.6 = f32[128,16,128]{2,0,1:T(8,128)S(1)} fusion(f32[128,16,128]{2,1,0:T(8,128)S(1)} %copy-done, s32[128]{0:T(128)S(1)} %iota_add_fusion.1), kind=kOutput, calls=%fused_computation.8 | convolution fusion | flops 402817024 | bytes 2097664 | tf_op jit(solution)/shard_map/dot_general | solution.py:18
  2.8 0.6 copy.24
  3.5 32.9 %all_to_all.36 = f32[128,16,128]{2,1,0:T(8,128)S(1)} all-to-all(f32[128,16,128]{2,1,0:T(8,128)S(1)} %copy.24), channel_id=1, replica_groups=mesh['row'=8,'col'=4] {'row'}, dimensions={0} | all-to-all | bytes 2097152 | tf_op jit(solution)/shard_map/all_to_all | solution.py:30
  36.3 0.1 copy.25
  36.4 2.0 %convolution_bitcast_fusion = f32[16,128,128]{1,2,0:T(8,128)S(1)} fusion(f32[16,128,128]{2,1,0:T(8,128)S(1)} %bitcast.21, s32[128]{0:T(128)S(1)} %iota_add_fusion.1), kind=kOutput, calls=%fused_computation.2 | convolution fusion | flops 402817024 | bytes 2097664 | tf_op jit(solution)/shard_map/dot_general | solution.py:18
  38.4 1.4 %copy.27 = f32[16,128,128]{2,0,1:T(8,128)} copy(f32[16,128,128]{1,2,0:T(8,128)S(1)} %convolution_bitcast_fusion) | data formatting | bytes 2097152 | tf_op jit(solution)/shard_map/transpose | solution.py:24
  39.8 3.7 %all-to-all-start.1 = ((f32[16,128,128]{2,0,1:T(8,128)}), f32[16,128,128]{2,0,1:T(8,128)S(1)}, u32[]{:S(2)}, u32[]{:S(2)}) async-start(f32[16,128,128]{2,0,1:T(8,128)} %copy.27), calls=%async_computation.1 | async-start | bytes 2097152 | tf_op jit(solution)/shard_map/all_to_all | solution.py:33
  43.5 0.0 copy-start.2
  43.5 0.6 copy-done.2
  44.2 0.1 dynamic_slice.7
  44.2 0.0 copy-start.3
  44.2 0.7 copy-done.3
  44.9 0.1 dynamic_slice.6
  45.0 0.1 broadcast_add_fusion
  45.0 12.7 %all-to-all-done.1 = f32[16,128,128]{2,0,1:T(8,128)S(1)} async-done(((f32[16,128,128]{2,0,1:T(8,128)}), f32[16,128,128]{2,0,1:T(8,128)S(1)}, u32[]{:S(2)}, u32[]{:S(2)}) %all-to-all-start.1) | async-done | bytes 1048608 | tf_op jit(solution)/shard_map/all_to_all | solution.py:33
  57.7 0.7 %copy.29 = f32[16,32,4,128]{3,2,1,0:T(4,128)S(1)} copy(f32[16,32,4,128]{3,0,1,2:T(8,128)S(1)} %bitcast.19) | data formatting | bytes 2097152 | tf_op jit(solution)/shard_map/all_to_all | solution.py:33
  58.4 0.0 copy-start.1
  58.4 0.4 all_to_all.33
  58.8 0.2 copy-done.1
  59.1 7.0 %convolution_multiply_fusion = f32[16,32,512]{2,1,0:T(8,128)} fusion(f32[16,32,512]{2,1,0:T(8,128)S(1)} %all_to_all.33, f32[512]{0:T(512)S(1)} %copy-done.1, f32[16,32]{1,0:T(8,128)S(1)} %broadcast_add_fusion, s32[512]{0:T(512)S(1)} %iota_add_fusion), kind=kOutput, calls=%fused_computation.1 | convolution fusion | flops 1614807040 | bytes 2103296 | tf_op jit(solution)/shard_map/dot_general | solution.py:18
  (2 shorter events, 0.0 us)
Async XLA Ops:
  0.0 1.2 %copy-start = (f32[128,16,128]{2,1,0:T(8,128)S(1)}, f32[128,16,128]{2,1,0:T(8,128)}, u32[]{:S(2)}) copy-start(f32[128,16,128]{2,1,0:T(8,128)} %param.4) | copy-start | bytes 3145732
  39.8 17.9 %all-to-all-start.1 = ((f32[16,128,128]{2,0,1:T(8,128)}), f32[16,128,128]{2,0,1:T(8,128)S(1)}, u32[]{:S(2)}, u32[]{:S(2)}) async-start(f32[16,128,128]{2,0,1:T(8,128)} %copy.27), calls=%async_computation.1 | async-start | bytes 2097152 | tf_op jit(solution)/shard_map/all_to_all | solution.py:33
  43.5 0.7 copy-start.2
  44.2 0.7 copy-start.3
  58.4 0.7 %copy-start.1 = (f32[512]{0:T(512)S(1)}, f32[512]{0:T(512)}, u32[]{:S(2)}) copy-start(f32[512]{0:T(512)} %param.7) | copy-start | bytes 6148
where the time goes:
time: 66.3 us; the launch traced here: 66 us
  blocking collectives  32.9 us (50%)
  waiting for transfers between devices  12.7 us (19%)
  matrix products  10.5 us (16%)
  local copies, waits for them, and re-layouts  6.11 us (9%)
  starting transfers between devices  3.7 us (6%)
    all_to_all x1, blocking collectives, per_device(): lax.all_to_all(part_values, 'row', split_axis=0, concat_axis=1, tiled=True)  32.9 us
    all_to_all x1, waiting for transfers between devices, per_device(): lax.all_to_all(local_values, 'col', split_axis=1, concat_axis=2, tiled=True)  12.7 us
    dot_general x3, matrix products, to_modes(): jnp.tensordot(values, transform_table(values.shape[dim]), axes=([dim], [0...  10.5 us
    all_to_all x1, starting transfers between devices, per_device(): lax.all_to_all(local_values, 'col', split_axis=1, concat_axis=2, tiled=True)  3.7 us
    unnamed x8, local copies, waits for them, and re-layouts  2.77 us
    transpose x1, local copies, waits for them, and re-layouts, to_modes(): return jnp.moveaxis(moved, -1, dim)  1.38 us
  transfers between devices with their start and end apart: 1, of which 1 were waited for; matrix products, arithmetic and copies ran while one was open for 0% of the time, Pallas kernels for 0%

commit v1 on v0

--- a/solution.py
+++ b/solution.py
@@ -30,7 +30,12 @@
     part_values = lax.all_to_all(part_values, "row", split_axis=0, concat_axis=1, tiled=True)
     part_values = to_modes(part_values, 1)
     local_values = part_values
-    local_values = lax.all_to_all(local_values, "col", split_axis=1, concat_axis=2, tiled=True)
+    local_values = jnp.concatenate(
+        lax.all_to_all(
+            jnp.stack(jnp.split(local_values, lax.axis_size("col"), axis=1)), "col", 0, 0
+        ),
+        axis=2,
+    )
     local_values = to_modes(local_values, 2)
     share_x = local_values.shape[0]
     part_x = lax.dynamic_slice_in_dim(symbol_x, lax.axis_index("row") * share_x, share_x)

time: 66.3 us -> 64.2 us (0.968)
  local copies, waits for them, and re-layouts: 6.11 us -> 3.48 us
  other arithmetic: 0.08 us -> 1.12 us
    transpose x1 -> x0, local copies, waits for them, and re-layouts: 1.38 us -> none  [to_modes(): return jnp.moveaxis(moved, -1, dim)]
    all_to_all x2 -> x0, local copies, waits for them, and re-layouts: 1.1 us -> none  [per_device(): lax.all_to_all(local_values, 'col', split_axis=1, concat_axis=2, tiled=True)]
    another operation x0 -> x1, other arithmetic: none -> 1.04 us  [per_device(): jnp.stack(jnp.split(local_values, lax.axis_size('col'), axis=1))]
where the time goes in v1:
time: 64.2 us; the launch traced here: 63.9 us
  blocking collectives  32.9 us (51%)
  waiting for transfers between devices  12.9 us (20%)
  matrix products  9.99 us (16%)
  starting transfers between devices  3.52 us (5%)
  local copies, waits for them, and re-layouts  3.48 us (5%)
  other arithmetic  1.12 us (2%)
    all_to_all x1, blocking collectives, per_device(): lax.all_to_all(part_values, 'row', split_axis=0, concat_axis=1, tiled=True)  32.9 us
    all_to_all x1, waiting for transfers between devices, per_device(): lax.all_to_all(jnp.stack(jnp.split(local_values, lax.axis_size('col'), ax...  12.9 us
    dot_general x3, matrix products, to_modes(): jnp.tensordot(values, transform_table(values.shape[dim]), axes=([dim], [0...  9.99 us
    all_to_all x1, starting transfers between devices, per_device(): lax.all_to_all(jnp.stack(jnp.split(local_values, lax.axis_size('col'), ax...  3.52 us
    unnamed x8, local copies, waits for them, and re-layouts  2.53 us
  transfers between devices with their start and end apart: 1, of which 1 were waited for; matrix products, arithmetic and copies ran while one was open for 0% of the time, Pallas kernels for 0%

profile of v1, /device:TPU:0, one launch (start us, length us, event | category | flops | bytes accessed | tf_op | source)
XLA Modules:
  0.0 63.9 jit_solution(8312727418267081878)
XLA Ops:
  0.0 0.0 copy-start
  0.0 1.2 %copy-done = f32[128,16,128]{2,1,0:T(8,128)S(1)} copy-done((f32[128,16,128]{2,1,0:T(8,128)S(1)}, f32[128,16,128]{2,1,0:T(8,128)}, u32[]{:S(2)}) %copy-start) | copy-done | bytes 1048600
  1.2 1.6 %fusion.8 = f32[128,16,128]{2,0,1:T(8,128)S(1)} fusion(f32[128,16,128]{2,1,0:T(8,128)S(1)} %copy-done, s32[128]{0:T(128)S(1)} %iota_add_fusion.1), kind=kOutput, calls=%fused_computation.11 | convolution fusion | flops 402817024 | bytes 2097664 | tf_op jit(solution)/shard_map/dot_general | solution.py:18
  2.8 0.6 copy.11
  3.4 32.9 %all_to_all.23 = f32[128,16,128]{2,1,0:T(8,128)S(1)} all-to-all(f32[128,16,128]{2,1,0:T(8,128)S(1)} %copy.11), channel_id=1, replica_groups=mesh['row'=8,'col'=4] {'row'}, dimensions={0} | all-to-all | bytes 2097152 | tf_op jit(solution)/shard_map/all_to_all | solution.py:30
  36.3 0.1 copy.12
  36.4 1.4 %convolution_bitcast_fusion = f32[16,128,128]{2,1,0:T(8,128)S(1)} fusion(f32[16,128,128]{2,1,0:T(8,128)S(1)} %bitcast.31, s32[128]{0:T(128)S(1)} %iota_add_fusion.1), kind=kOutput, calls=%fused_computation.2 | convolution fusion | flops 402817024 | bytes 2097664 | tf_op jit(solution)/shard_map/dot_general | solution.py:18
  37.9 0.1 slice_bitcast_fusion.3
  38.0 1.0 %pad_maximum_fusion = f32[4,16,32,128]{3,2,1,0:T(8,128)} fusion(f32[1,16,32,128]{3,2,1,0:T(8,128)S(1)} %get-tuple-element.6, f32[1,16,32,128]{3,2,1,0:T(8,128)S(1)} %get-tuple-element.7, f32[1,16,32,128]{3,2,1,0:T(8,128)S(1)} %get-tuple-element.8, f32[1,16,32,128]{3,2,1,0:T(8,128)S(1)} %get-tuple-element.5), kind=kLoop, calls=%fused_computation.10 | loop fusion | flops 786432 | bytes 2097152 | tf_op jit(solution)/shard_map/stack | solution.py:35
  39.0 3.5 %all-to-all-start.1 = ((f32[4,16,32,128]{3,2,1,0:T(8,128)}), f32[4,16,32,128]{3,2,1,0:T(8,128)S(1)}, u32[]{:S(2)}, u32[]{:S(2)}) async-start(f32[4,16,32,128]{3,2,1,0:T(8,128)} %pad_maximum_fusion), calls=%async_computation.1 | async-start | bytes 2097152 | tf_op jit(solution)/shard_map/all_to_all | solution.py:34
  42.5 0.0 copy-start.2
  42.5 0.6 %copy-done.2 = f32[128]{0:T(128)S(1)} copy-done((f32[128]{0:T(128)S(1)}, f32[128]{0:T(128)}, u32[]{:S(2)}) %copy-start.2) | copy-done | bytes 536
  43.2 0.1 dynamic_slice.6
  43.3 0.0 copy-start.3
  43.3 0.7 %copy-done.3 = f32[128]{0:T(128)S(1)} copy-done((f32[128]{0:T(128)S(1)}, f32[128]{0:T(128)}, u32[]{:S(2)}) %copy-start.3) | copy-done | bytes 536
  43.9 0.1 dynamic_slice.7
  44.0 0.0 copy-start.1
  44.0 0.1 broadcast_add_fusion
  44.1 12.9 %all-to-all-done.1 = f32[4,16,32,128]{3,2,1,0:T(8,128)S(1)} async-done(((f32[4,16,32,128]{3,2,1,0:T(8,128)}), f32[4,16,32,128]{3,2,1,0:T(8,128)S(1)}, u32[]{:S(2)}, u32[]{:S(2)}) %all-to-all-start.1) | async-done | bytes 1048608 | tf_op jit(solution)/shard_map/all_to_all | solution.py:34
  56.9 0.0 copy-done.1
  56.9 7.0 %convolution_multiply_fusion = f32[16,32,512]{2,1,0:T(8,128)} fusion(f32[512]{0:T(512)S(1)} %copy-done.1, f32[16,32]{1,0:T(8,128)S(1)} %broadcast_add_fusion, s32[512]{0:T(512)S(1)} %iota_add_fusion, f32[4,16,32,128]{3,2,1,0:T(8,128)S(1)} %all-to-all-done.1), kind=kOutput, calls=%fused_computation.1 | convolution fusion | flops 1614807040 | bytes 2103296 | tf_op jit(solution)/shard_map/dot_general | solution.py:18
  (2 shorter events, 0.0 us)
Async XLA Ops:
  0.0 1.2 %copy-start = (f32[128,16,128]{2,1,0:T(8,128)S(1)}, f32[128,16,128]{2,1,0:T(8,128)}, u32[]{:S(2)}) copy-start(f32[128,16,128]{2,1,0:T(8,128)} %param.4) | copy-start | bytes 3145732
  39.0 17.9 %all-to-all-start.1 = ((f32[4,16,32,128]{3,2,1,0:T(8,128)}), f32[4,16,32,128]{3,2,1,0:T(8,128)S(1)}, u32[]{:S(2)}, u32[]{:S(2)}) async-start(f32[4,16,32,128]{3,2,1,0:T(8,128)} %pad_maximum_fusion), calls=%async_computation.1 | async-start | bytes 2097152 | tf_op jit(solution)/shard_map/all_to_all | solution.py:34
  42.5 0.7 %copy-start.2 = (f32[128]{0:T(128)S(1)}, f32[128]{0:T(128)}, u32[]{:S(2)}) copy-start(f32[128]{0:T(128)} %param.5) | copy-start | bytes 1540
  43.3 0.7 %copy-start.3 = (f32[128]{0:T(128)S(1)}, f32[128]{0:T(128)}, u32[]{:S(2)}) copy-start(f32[128]{0:T(128)} %param.6) | copy-start | bytes 1540
  44.0 12.9 %copy-start.1 = (f32[512]{0:T(512)S(1)}, f32[512]{0:T(512)}, u32[]{:S(2)}) copy-start(f32[512]{0:T(512)} %param.7) | copy-start | bytes 6148
